TPU v7x, 32 devices: a whole 2x2x4 slice. The times are simulated.
32 devices in a mesh: lat: 4 (over z), lon: 8 (over y, x, core).
Axes of the slice: x: 2, y: 2, z: 4, core: 2. Of those that a mesh axis runs over, the one named last changes fastest.
Arguments:
- observations: bfloat16 [49152, 128], P(('lat', 'lon')), may hold values from -6 to 6
- owner_device: int32 [49152, 1], P(('lat', 'lon')), may hold values from 0 to 31; in each aligned block of 1536 rows (0 to 1535, 1536 to 3071, ...) at most 96 rows name the same one
- local_cell: int32 [49152], P(('lat', 'lon')), may hold values from 0 to 383
- valid_counts: int32 [32], P(('lat', 'lon')), may hold values from 768 to 1536
- weight_in: bfloat16 [128, 256], replicated, may hold values from -0.5 to 0.5
- bias_in: float32 [256], replicated, may hold values from -3 to 3
- weight_out: bfloat16 [256, 256], replicated, may hold values from -0.375 to 0.375
- kernel_taps: float32 [9, 256], replicated, may hold values from -2 to 2
- cotangent: bfloat16 [64, 192, 256], P(('lat', 'lon')), may hold values from -6 to 6
Outputs:
- grid_out: bfloat16 [64, 192, 256], P(('lat', 'lon'))
- grad_weight_in: float32 [128, 256], replicated
- grad_bias_in: float32 [256], replicated
- grad_weight_out: float32 [256, 256], replicated
- grad_kernel: float32 [9, 256], replicated
Inputs may be any that keep to these rules, and one draw needn't show every extreme that they name: `owner_device`: within the rows of one block, at most 96 rows name one owner, and in every draw some block names some owner exactly 96 times.
All inputs are finite; a program needn't handle non-finite values.
Results may differ from a plain program's by a relative error of at most 0.0065.
Values may be sent and summed in bfloat16 or wider, within the bound.
A program may use at most 64 MiB of HBM per device.

v0:
```python
import math
import jax
import jax.numpy as jnp
from jax import lax
from jax.sharding import PartitionSpec as P

OFFSETS = [(shift_lat, shift_lon) for shift_lat in (-1, 0, 1) for shift_lon in (-1, 0, 1)]


def extended(shard, sides, width):
    for axis, dim in sides:
        count, length = (lax.axis_size(axis), shard.shape[dim])
        up = [(i, (i + 1) % count) for i in range(count)]
        down = [(j, i) for i, j in up]
        last = lax.slice_in_dim(shard, length - width, length, axis=dim)
        first = lax.slice_in_dim(shard, 0, width, axis=dim)
        before = lax.ppermute(last, axis, up)
        after = lax.ppermute(first, axis, down)
        shard = jnp.concatenate([before, shard, after], axis=dim)
    return shard


def encoder(rows, weight_in, bias_in, weight_out):
    before = jnp.dot(rows, weight_in, preferred_element_type=jnp.float32) + bias_in
    hidden = jax.nn.gelu(before).astype(jnp.bfloat16)
    encoded = jnp.dot(hidden, weight_out, preferred_element_type=jnp.float32).astype(jnp.bfloat16)
    return (before, hidden, encoded)


def local_grads(rows, before, hidden, upstream, weight_out):
    contract = (((0,), (0,)), ((), ()))
    grad_out = lax.dot_general(hidden, upstream, contract, preferred_element_type=jnp.float32)
    back = lax.dot_general(
        upstream, weight_out, (((1,), (1,)), ((), ())), preferred_element_type=jnp.float32
    )
    _, pullback = jax.vjp(jax.nn.gelu, before)
    pre_grad = pullback(back)[0].astype(jnp.bfloat16)
    grad_in = lax.dot_general(rows, pre_grad, contract, preferred_element_type=jnp.float32)
    grad_bias = jnp.sum(pre_grad.astype(jnp.float32), axis=0)
    return (grad_in, grad_bias, grad_out)


def edge_mask(padded, tile_rows):
    lat_count = lax.axis_size("lat")
    lat_here = lax.axis_index("lat")
    row_ids = jnp.arange(tile_rows + 2, dtype=jnp.int32)
    outside = (row_ids == 0) & (lat_here == 0) | (row_ids == tile_rows + 1) & (
        lat_here == lat_count - 1
    )
    keep_rows = jnp.logical_not(outside).astype(padded.dtype)
    return padded * keep_rows[:, None, None]


def local(
    observations,
    owner_device,
    local_cell,
    valid_counts,
    weight_in,
    bias_in,
    weight_out,
    kernel_taps,
    cotangent,
):
    lat_count = lax.axis_size("lat")
    lon_count = lax.axis_size("lon")
    devices_all = lat_count * lon_count
    obs_rows = observations.shape[0]
    channels = weight_out.shape[1]
    capacity = 2 * obs_rows // devices_all
    tile_rows = cotangent.shape[0] * lon_count
    tile_cols = cotangent.shape[1] // lon_count
    cells_tile = tile_rows * tile_cols
    owners = owner_device[:, 0]
    valid_rows = jnp.arange(obs_rows, dtype=jnp.int32) < valid_counts[0]
    matches = (owners[:, None] == jnp.arange(devices_all, dtype=jnp.int32)[None, :]).astype(
        jnp.int32
    )
    earlier = jnp.sum((jnp.cumsum(matches, axis=0) - 1) * matches, axis=1)
    slot_index = owners * capacity + earlier
    sent_cells = jnp.full((devices_all * capacity,), cells_tile, jnp.int32)
    sent_cells = sent_cells.at[slot_index].set(jnp.where(valid_rows, local_cell, cells_tile))
    got_cells = lax.all_to_all(
        sent_cells.reshape(devices_all, capacity),
        ("lat", "lon"),
        split_axis=0,
        concat_axis=0,
        tiled=True,
    ).reshape(-1)
    width = observations.shape[1]
    outgoing = (
        jnp.zeros((devices_all * capacity, width), observations.dtype)
        .at[slot_index]
        .set(observations)
    )
    arrived = lax.all_to_all(
        outgoing.reshape(devices_all, capacity, width),
        ("lat", "lon"),
        split_axis=0,
        concat_axis=0,
        tiled=True,
    )
    arrived_rows = arrived.reshape(devices_all * capacity, width)
    before, hidden, arrived_enc = encoder(arrived_rows, weight_in, bias_in, weight_out)
    deposit = jax.ops.segment_sum(
        arrived_enc.astype(jnp.float32), got_cells, num_segments=cells_tile + 1
    )
    deposit = deposit[:cells_tile].reshape(tile_rows, tile_cols, channels)
    padded = extended(deposit, (("lat", 0), ("lon", 1)), 1)
    padded = edge_mask(padded, tile_rows)
    grid_field = jnp.zeros((tile_rows, tile_cols, channels), jnp.float32)
    for tap_index, (shift_lat, shift_lon) in enumerate(OFFSETS):
        window = padded[
            1 + shift_lat : 1 + shift_lat + tile_rows, 1 + shift_lon : 1 + shift_lon + tile_cols
        ]
        grid_field = grid_field + kernel_taps[tap_index] * window
    grid_out = lax.all_to_all(
        grid_field.astype(jnp.bfloat16), "lon", split_axis=0, concat_axis=1, tiled=True
    )
    loss_scale = 1.0 / math.sqrt(obs_rows * devices_all)
    cot_tile = lax.all_to_all(cotangent, "lon", split_axis=1, concat_axis=0, tiled=True)
    cot_float = cot_tile.astype(jnp.float32)
    cot_padded = extended(cot_tile, (("lat", 0), ("lon", 1)), 1)
    cot_padded = edge_mask(cot_padded, tile_rows).astype(jnp.float32)
    kernel_rows = []
    adjoint = jnp.zeros((tile_rows, tile_cols, channels), jnp.float32)
    for tap_index, (shift_lat, shift_lon) in enumerate(OFFSETS):
        window = padded[
            1 + shift_lat : 1 + shift_lat + tile_rows, 1 + shift_lon : 1 + shift_lon + tile_cols
        ]
        kernel_rows.append(loss_scale * jnp.sum(cot_float * window, axis=(0, 1)))
        back_window = cot_padded[
            1 - shift_lat : 1 - shift_lat + tile_rows, 1 - shift_lon : 1 - shift_lon + tile_cols
        ]
        adjoint = adjoint + kernel_taps[tap_index] * back_window
    grad_kernel = jnp.stack(kernel_rows)
    adjoint = (loss_scale * adjoint).astype(jnp.bfloat16)
    adjoint_rows = jnp.concatenate(
        [adjoint.reshape(cells_tile, channels), jnp.zeros((1, channels), jnp.bfloat16)], axis=0
    )
    upstream = adjoint_rows[got_cells]
    grads = local_grads(arrived_rows, before, hidden, upstream, weight_out)
    grad_in, grad_bias, grad_out, grad_kernel = lax.psum(
        (grads[0], grads[1], grads[2], grad_kernel), ("lat", "lon")
    )
    return (grid_out, grad_in, grad_bias, grad_out, grad_kernel)


def solution(mesh):
    return jax.shard_map(
        local,
        mesh=mesh,
        in_specs=(
            P(("lat", "lon"), None),
            P(("lat", "lon"), None),
            P(("lat", "lon")),
            P(("lat", "lon")),
            P(),
            P(),
            P(),
            P(),
            P(("lat", "lon"), None, None),
        ),
        out_specs=(P(("lat", "lon"), None, None), P(), P(), P(), P()),
        check_vma=False,
    )
```

profile of v0, /device:TPU:0, one launch (start us, length us, event | category | flops | bytes accessed | tf_op | source)
XLA Modules:
  0.0 271.2 jit_solution(18164300997538134326)
XLA Ops:
  8.6 9.1 %reduce-window.6 = s32[32,12,128]{2,1,0:T(8,128)S(1)} reduce-window(s32[32,12,128]{2,1,0:T(8,128)S(1)} %fusion.30, s32[]{:T(128)} %constant.21.clone.1), window={size=1x1x128 pad=0_0x0_0x127_0}, to_apply=%region_0.0 | reduce-window | flops 6242304 | bytes 393220 | tf_op jit(solution)/shard_map/reduce-window
  19.8 6.2 %scatter_custom_fusion = s32[3072]{0:T(1024)S(1)} fusion(s32[1536]{0:T(1024)S(1)} %fusion.36, s32[1536]{0:T(1024)S(1)} %fusion.35, s32[]{:T(128)} %constant.19.clone.1), kind=kCustom, calls=%fused_computation.84 | custom fusion | bytes 12292 | tf_op jit(solution)/shard_map/scatter | solution.py:82
  26.7 7.3 %all-to-all-start = ((s32[32,1,96]{2,1,0:T(1,128)}), s32[32,1,96]{2,1,0:T(1,128)S(1)}, u32[]{:S(2)}, u32[]{:S(2)}) async-start(s32[32,1,96]{2,1,0:T(1,128)} %all_to_all.35), calls=%async_computation | async-start | bytes 32768 | tf_op jit(solution)/shard_map/all_to_all | solution.py:83
  34.1 1.8 copy.23
  35.9 5.7 %scatter_custom_fusion.1 = bf16[3072,128]{1,0:T(8,128)(2,1)} fusion(s32[1536]{0:T(1024)S(1)} %fusion.36, bf16[1536,128]{1,0:T(8,128)(2,1)} %param.9, bf16[]{:T(256)} %constant.24.clone.1), kind=kCustom, calls=%fused_computation.57 | custom fusion | bytes 786944 | tf_op jit(solution)/shard_map/scatter | solution.py:94
  41.6 3.9 %all-to-all-start.3 = ((bf16[2,192,256]{2,0,1:T(2,128)(2,1)}), bf16[2,192,256]{2,0,1:T(2,128)(2,1)S(1)}, u32[]{:S(2)}, u32[]{:S(2)}) async-start(bf16[2,192,256]{2,0,1:T(2,128)(2,1)} %copy.23), calls=%async_computation.3 | async-start | bytes 393216 | tf_op jit(solution)/shard_map/all_to_all | solution.py:121
  45.7 6.1 %all-to-all-done.3 = bf16[2,192,256]{2,0,1:T(2,128)(2,1)S(1)} async-done(((bf16[2,192,256]{2,0,1:T(2,128)(2,1)}), bf16[2,192,256]{2,0,1:T(2,128)(2,1)S(1)}, u32[]{:S(2)}, u32[]{:S(2)}) %all-to-all-start.3) | async-done | bytes 196640 | tf_op jit(solution)/shard_map/all_to_all | solution.py:121
  51.8 3.7 %all-to-all-start.1 = ((bf16[32,96,128]{2,1,0:T(8,128)(2,1)}), bf16[32,96,128]{2,1,0:T(8,128)(2,1)S(1)}, u32[]{:S(2)}, u32[]{:S(2)}) async-start(bf16[32,96,128]{2,1,0:T(8,128)(2,1)} %bitcast.4), calls=%async_computation.1 | async-start | bytes 1572864 | tf_op jit(solution)/shard_map/all_to_all | solution.py:96
  55.6 1.8 collective-permute-start.4
  57.4 2.1 collective-permute-start.5
  59.5 13.7 %collective-permute-done.4 = bf16[1,24,256]{2,1,0:T(8,128)(2,1)S(1)} collective-permute-done((bf16[1,24,256]{2,1,0:T(8,128)(2,1)S(1)}, bf16[1,24,256]{2,1,0:T(8,128)(2,1)S(1)}, u32[]{:S(2)}, u32[]{:S(2)}) %collective-permute-start.4) | collective-permute-done | bytes 12320 | tf_op jit(solution)/shard_map/ppermute | solution.py:17
  73.3 2.6 collective-permute-start.7
  77.9 11.1 %gather_fusion = bf16[3072,256]{1,0:T(8,128)(2,1)S(1)} fusion(bf16[385,256]{1,0:T(8,128)(2,1)S(1)} %concatenate.19, s32[3072]{0:T(1024)S(1)} %broadcast_clamp_fusion), kind=kCustom, calls=%fused_computation | custom fusion | bytes 3158016 | tf_op jit(solution)/shard_map/gather | solution.py:141
  89.0 2.3 fusion.45
  91.3 5.0 %convert_reduce_fusion = (f32[256]{0:T(256)S(1)}, bf16[3072,256]{1,0:T(8,128)(2,1)}, f32[3072,256]{1,0:T(8,128)S(1)}) fusion(f32[3072,256]{1,0:T(8,128)} %fusion.45, f32[256]{0:T(256)S(1)} %copy-done.4, bf16[3072,128]{1,0:T(8,128)(2,1)S(1)} %bitcast.78, bf16[128,256]{1,0:T(8,128)(2,1)S(1)} %copy-done.3), kind=kOutput, calls=%fused_computation.16 | convolution fusion | flops 219414272 | bytes 8718336 | tf_op jit(solution)/shard_map/dot_general | solution.py:24
  97.9 2.8 %fusion = f32[3072,256]{1,0:T(8,128)} fusion(bf16[256,256]{1,0:T(8,128)(2,1)S(1)} %copy-done, f32[3072,256]{1,0:T(8,128)S(1)} %get-tuple-element.37), kind=kOutput, calls=%fused_computation.8 | convolution fusion | flops 411303936 | bytes 6422528 | tf_op jit(solution)/shard_map/dot_general | solution.py:26
  100.7 19.6 %scatter_custom_fusion.2 = f32[385,256]{1,0:T(8,128)S(1)} fusion(s32[3072]{0:T(1024)S(1)} %reshape.214, f32[3072,256]{1,0:T(8,128)} %fusion, f32[]{:T(128)} %constant.18.clone.1), kind=kCustom, calls=%fused_computation.64 | custom fusion | flops 786432 | bytes 394752 | tf_op jit(solution)/shard_map/scatter-add | solution.py:105
  120.4 4.8 %collective-permute-start = (f32[1,24,256]{2,1,0:T(8,128)S(1)}, f32[1,24,256]{2,1,0:T(8,128)S(1)}, u32[]{:S(2)}, u32[]{:S(2)}) collective-permute-start(f32[1,24,256]{2,1,0:T(8,128)S(1)} %get-tuple-element.22), channel_id=1, source_target_pairs={{0,8},{8,16},{16,24},{24,0},{1,9},{9,17},{17,25},{25,1},{2,10},{10... | collective-permute-start | bytes 73736 | tf_op jit(solution)/shard_map/ppermute | solution.py:17
  125.2 3.9 %fusion.41 = f32[256,256]{1,0:T(8,128)} fusion(bf16[3072,256]{1,0:T(8,128)(2,1)S(1)} %gather_fusion, f32[3072,256]{1,0:T(8,128)} %copy-done.5), kind=kOutput, calls=%fused_computation.98 | convolution fusion | flops 409731072 | bytes 4980736 | tf_op jit(solution)/shard_map/dot_general | solution.py:32
  129.2 2.6 collective-permute-start.3
  134.7 3.9 %all-to-all-start.2 = ((bf16[16,24,256]{2,1,0:T(8,128)(2,1)}), bf16[16,24,256]{2,1,0:T(8,128)(2,1)S(1)}, u32[]{:S(2)}, u32[]{:S(2)}) async-start(bf16[16,24,256]{2,1,0:T(8,128)(2,1)} %add_convert_fusion), calls=%async_computation.2 | async-start | bytes 393216 | tf_op jit(solution)/shard_map/all_to_all | solution.py:117
  138.7 41.4 %all-reduce.1 = (f32[256]{0:T(256)}, f32[9,256]{1,0:T(8,128)}) all-reduce(f32[256]{0:T(256)S(1)} %get-tuple-element.18, f32[9,256]{1,0:T(8,128)S(1)} %stack.2), channel_id=1, replica_groups=mesh['lat'=4,'lon'=8] {'lat','lon'}, use_global_device_ids=true, to_apply=%region_8.9 | all-reduce | flops 2560 | bytes 20480 | tf_op jit(solution)/shard_map/psum | solution.py:143
  180.9 80.2 %all-reduce.5.cloned.1.call-done = (f32[128,256]{1,0:T(8,128)}, f32[256,256]{1,0:T(8,128)}) async-done(((f32[128,256]{1,0:T(8,128)}, f32[256,256]{1,0:T(8,128)}), (f32[128,256]{1,0:T(8,128)}, f32[256,256]{1,0:T(8,128)})) %all-reduce.5.cloned.1.call-update) | async-done | bytes 393232 | tf_op jit(solution)/shard_map/psum | solution.py:143
  262.7 1.7 copy.31
  (68 shorter events, 12.7 us)
Async XLA Ops:
  7.2 81.8 %copy-start = (bf16[256,256]{1,0:T(8,128)(2,1)S(1)}, bf16[256,256]{1,0:T(8,128)(2,1)}, u32[]{:S(2)}) copy-start(bf16[256,256]{1,0:T(8,128)(2,1)} %param.15) | copy-start | bytes 393220
  7.2 38.4 %copy-start.2 = (f32[9,256]{1,0:T(8,128)S(1)}, f32[9,256]{1,0:T(8,128)}, u32[]{:S(2)}) copy-start(f32[9,256]{1,0:T(8,128)} %param.16) | copy-start | bytes 27652
  26.7 14.9 %all-to-all-start = ((s32[32,1,96]{2,1,0:T(1,128)}), s32[32,1,96]{2,1,0:T(1,128)S(1)}, u32[]{:S(2)}, u32[]{:S(2)}) async-start(s32[32,1,96]{2,1,0:T(1,128)} %all_to_all.35), calls=%async_computation | async-start | bytes 32768 | tf_op jit(solution)/shard_map/all_to_all | solution.py:83
  41.6 10.1 %all-to-all-start.3 = ((bf16[2,192,256]{2,0,1:T(2,128)(2,1)}), bf16[2,192,256]{2,0,1:T(2,128)(2,1)S(1)}, u32[]{:S(2)}, u32[]{:S(2)}) async-start(bf16[2,192,256]{2,0,1:T(2,128)(2,1)} %copy.23), calls=%async_computation.3 | async-start | bytes 393216 | tf_op jit(solution)/shard_map/all_to_all | solution.py:121
  51.8 39.5 %all-to-all-start.1 = ((bf16[32,96,128]{2,1,0:T(8,128)(2,1)}), bf16[32,96,128]{2,1,0:T(8,128)(2,1)S(1)}, u32[]{:S(2)}, u32[]{:S(2)}) async-start(bf16[32,96,128]{2,1,0:T(8,128)(2,1)} %bitcast.4), calls=%async_computation.1 | async-start | bytes 1572864 | tf_op jit(solution)/shard_map/all_to_all | solution.py:96
  55.5 205.6 %all-reduce.5.cloned.1.call-start = ((), (), s32[]{:S(2)}) async-start(), calls=%async_computation.4 | async-start | bytes 786432 | tf_op jit(solution)/shard_map/psum | solution.py:143
  55.6 17.6 %collective-permute-start.4 = (bf16[1,24,256]{2,1,0:T(8,128)(2,1)S(1)}, bf16[1,24,256]{2,1,0:T(8,128)(2,1)S(1)}, u32[]{:S(2)}, u32[]{:S(2)}) collective-permute-start(bf16[1,24,256]{2,1,0:T(8,128)(2,1)S(1)} %get-tuple-element.26), channel_id=1, source_target_pairs={{0,8},{8,16},{16,24},{24,0},{1,9},{9,17},{17,25},{25,1},{2,10},{10... | collective-permute-start | bytes 36872 | tf_op jit(solution)/shard_map/ppermute | solution.py:17
  57.4 15.8 %collective-permute-start.5 = (bf16[1,24,256]{2,1,0:T(8,128)(2,1)S(1)}, bf16[1,24,256]{2,1,0:T(8,128)(2,1)S(1)}, u32[]{:S(2)}, u32[]{:S(2)}) collective-permute-start(bf16[1,24,256]{2,1,0:T(8,128)(2,1)S(1)} %get-tuple-element.27), channel_id=1, source_target_pairs={{8,0},{16,8},{24,16},{0,24},{9,1},{17,9},{25,17},{1,25},{10,2},{18... | collective-permute-start | bytes 36872 | tf_op jit(solution)/shard_map/ppermute | solution.py:18
  73.3 4.1 %collective-permute-start.6 = (bf16[18,1,256]{2,1,0:T(2,128)(2,1)S(1)}, bf16[18,1,256]{2,1,0:T(2,128)(2,1)S(1)}, u32[]{:S(2)}, u32[]{:S(2)}) collective-permute-start(bf16[18,1,256]{2,1,0:T(2,128)(2,1)S(1)} %get-tuple-element.24), channel_id=1, source_target_pairs={{0,1},{1,2},{2,3},{3,4},{4,5},{5,6},{6,7},{7,0},{8,9},{9,10},{10,1... | collective-permute-start | bytes 27656 | tf_op jit(solution)/shard_map/ppermute | solution.py:17
  73.3 4.1 %collective-permute-start.7 = (bf16[18,1,256]{2,1,0:T(2,128)(2,1)S(1)}, bf16[18,1,256]{2,1,0:T(2,128)(2,1)S(1)}, u32[]{:S(2)}, u32[]{:S(2)}) collective-permute-start(bf16[18,1,256]{2,1,0:T(2,128)(2,1)S(1)} %get-tuple-element.25), channel_id=1, source_target_pairs={{1,0},{2,1},{3,2},{4,3},{5,4},{6,5},{7,6},{0,7},{9,8},{10,9},{11,1... | collective-permute-start | bytes 27656 | tf_op jit(solution)/shard_map/ppermute | solution.py:18
  89.0 2.3 copy-start.3
  89.0 2.3 copy-start.4
  96.2 1.7 copy-start.5
  120.4 8.7 %collective-permute-start = (f32[1,24,256]{2,1,0:T(8,128)S(1)}, f32[1,24,256]{2,1,0:T(8,128)S(1)}, u32[]{:S(2)}, u32[]{:S(2)}) collective-permute-start(f32[1,24,256]{2,1,0:T(8,128)S(1)} %get-tuple-element.22), channel_id=1, source_target_pairs={{0,8},{8,16},{16,24},{24,0},{1,9},{9,17},{17,25},{25,1},{2,10},{10... | collective-permute-start | bytes 73736 | tf_op jit(solution)/shard_map/ppermute | solution.py:17
  125.2 6.7 %copy-start.1 = (bf16[3072,256]{1,0:T(8,128)(2,1)S(1)}, bf16[3072,256]{1,0:T(8,128)(2,1)}, u32[]{:S(2)}) copy-start(bf16[3072,256]{1,0:T(8,128)(2,1)} %get-tuple-element.19) | copy-start | bytes 4718596
  125.2 3.9 %collective-permute-start.1 = (f32[1,24,256]{2,1,0:T(8,128)S(1)}, f32[1,24,256]{2,1,0:T(8,128)S(1)}, u32[]{:S(2)}, u32[]{:S(2)}) collective-permute-start(f32[1,24,256]{2,1,0:T(8,128)S(1)} %get-tuple-element.23), channel_id=1, source_target_pairs={{8,0},{16,8},{24,16},{0,24},{9,1},{17,9},{25,17},{1,25},{10,2},{18... | collective-permute-start | bytes 73736 | tf_op jit(solution)/shard_map/ppermute | solution.py:18
  129.2 4.1 %collective-permute-start.2 = (f32[18,1,256]{2,1,0:T(1,128)S(1)}, f32[18,1,256]{2,1,0:T(1,128)S(1)}, u32[]{:S(2)}, u32[]{:S(2)}) collective-permute-start(f32[18,1,256]{2,1,0:T(1,128)S(1)} %get-tuple-element.20), channel_id=1, source_target_pairs={{0,1},{1,2},{2,3},{3,4},{4,5},{5,6},{6,7},{7,0},{8,9},{9,10},{10,1... | collective-permute-start | bytes 55304 | tf_op jit(solution)/shard_map/ppermute | solution.py:17
  129.2 4.1 %collective-permute-start.3 = (f32[18,1,256]{2,1,0:T(1,128)S(1)}, f32[18,1,256]{2,1,0:T(1,128)S(1)}, u32[]{:S(2)}, u32[]{:S(2)}) collective-permute-start(f32[18,1,256]{2,1,0:T(1,128)S(1)} %get-tuple-element.21), channel_id=1, source_target_pairs={{1,0},{2,1},{3,2},{4,3},{5,4},{6,5},{7,6},{0,7},{9,8},{10,9},{11,1... | collective-permute-start | bytes 55304 | tf_op jit(solution)/shard_map/ppermute | solution.py:18
  134.7 45.4 %all-to-all-start.2 = ((bf16[16,24,256]{2,1,0:T(8,128)(2,1)}), bf16[16,24,256]{2,1,0:T(8,128)(2,1)S(1)}, u32[]{:S(2)}, u32[]{:S(2)}) async-start(bf16[16,24,256]{2,1,0:T(8,128)(2,1)} %add_convert_fusion), calls=%async_computation.2 | async-start | bytes 393216 | tf_op jit(solution)/shard_map/all_to_all | solution.py:117
Sparse Core Ops, SparseCore 0:
  133.1 127.9 all-reduce.4
where the time goes:
time: 272 us; the launch traced here: 271 us
  waiting for transfers between devices  101 us (37%)
  blocking collectives  41.4 us (15%)
  other arithmetic  33.8 us (12%)
  starting transfers between devices  33 us (12%)
  local copies, waits for them, and re-layouts  32.3 us (12%)
  matrix products  15 us (6%)
  between operations  15 us (6%)
    psum x1, waiting for transfers between devices, local(): lax.psum((grads[0], grads[1], grads[2], grad_kernel), ('lat', 'lon'))  80.2 us
    psum x1, blocking collectives, local(): lax.psum((grads[0], grads[1], grads[2], grad_kernel), ('lat', 'lon'))  41.4 us
    scatter-add x1, other arithmetic, local(): jax.ops.segment_sum(arrived_enc.astype(jnp.float32), got_cells, num_segme...  19.6 us
    ppermute x4, waiting for transfers between devices, extended(): before = lax.ppermute(last, axis, up)  14.2 us
    gather x1, local copies, waits for them, and re-layouts, local(): upstream = adjoint_rows[got_cells]  11.1 us
    another operation x2, other arithmetic  9.11 us
    all_to_all x1, starting transfers between devices, local(): lax.all_to_all(sent_cells.reshape(devices_all, capacity), ('lat', 'lon'),...  7.33 us
    ppermute x4, starting transfers between devices, extended(): after = lax.ppermute(first, axis, down)  7.32 us
  transfers between devices with their start and end apart: 13, of which 5 were waited for; matrix products, arithmetic and copies ran while one was open for 11% of the time, Pallas kernels for 0%

commit v1 on v0

--- a/solution.py
+++ b/solution.py
@@ -141,7 +141,7 @@
     upstream = adjoint_rows[got_cells]
     grads = local_grads(arrived_rows, before, hidden, upstream, weight_out)
     grad_in, grad_bias, grad_out, grad_kernel = lax.psum(
-        (grads[0], grads[1], grads[2], grad_kernel), ("lat", "lon")
+        lax.psum((grads[0], grads[1], grads[2], grad_kernel), "lon"), "lat"
     )
     return (grid_out, grad_in, grad_bias, grad_out, grad_kernel)
 

time: 272 us -> 241 us (0.89)
  waiting for transfers between devices: 101 us -> 68.3 us
    psum x1 -> x2, waiting for transfers between devices: 80.2 us -> 47.9 us  [the longest x1 47.9 us: local(): lax.psum((grads[0], grads[1], grads[2], grad_kernel), 'lon')]
    psum x1 -> x2, blocking collectives: 41.4 us -> 42.5 us  [the longest x1 22.4 us: local(): lax.psum((grads[0], grads[1], grads[2], grad_kernel), 'lon')]
  transfers between devices with their start and end apart: 13 -> 14, of which waited for: 5 -> 5; matrix products, arithmetic and copies ran while one was open for 11% -> 12% of each run, Pallas kernels for 0% -> 0%
where the time goes in v1:
time: 241 us; the launch traced here: 240 us
  waiting for transfers between devices  68.3 us (28%)
  blocking collectives  42.5 us (18%)
  other arithmetic  33.8 us (14%)
  starting transfers between devices  33 us (14%)
  local copies, waits for them, and re-layouts  32.3 us (13%)
  matrix products  15 us (6%)
  between operations  15 us (6%)
    psum x1, waiting for transfers between devices, local(): lax.psum((grads[0], grads[1], grads[2], grad_kernel), 'lon')  47.9 us
    psum x1, blocking collectives, local(): lax.psum((grads[0], grads[1], grads[2], grad_kernel), 'lon')  22.4 us
    psum x1, blocking collectives, local(): lax.psum(lax.psum((grads[0], grads[1], grads[2], grad_kernel), 'lon'), 'l...  20.1 us
    scatter-add x1, other arithmetic, local(): jax.ops.segment_sum(arrived_enc.astype(jnp.float32), got_cells, num_segme...  19.6 us
    ppermute x4, waiting for transfers between devices, extended(): before = lax.ppermute(last, axis, up)  14.2 us
    gather x1, local copies, waits for them, and re-layouts, local(): upstream = adjoint_rows[got_cells]  11.1 us
    another operation x2, other arithmetic  9.11 us
    all_to_all x1, starting transfers between devices, local(): lax.all_to_all(sent_cells.reshape(devices_all, capacity), ('lat', 'lon'),...  7.33 us
  transfers between devices with their start and end apart: 14, of which 5 were waited for; matrix products, arithmetic and copies ran while one was open for 12% of the time, Pallas kernels for 0%

profile of v1, /device:TPU:0, one launch (start us, length us, event | category | flops | bytes accessed | tf_op | source)
XLA Modules:
  0.0 240.0 jit_solution(10202258912781663699)
XLA Ops:
  8.6 9.1 %reduce-window.6 = s32[32,12,128]{2,1,0:T(8,128)S(1)} reduce-window(s32[32,12,128]{2,1,0:T(8,128)S(1)} %fusion.30, s32[]{:T(128)} %constant.21.clone.1), window={size=1x1x128 pad=0_0x0_0x127_0}, to_apply=%region_0.0 | reduce-window | flops 6242304 | bytes 393220 | tf_op jit(solution)/shard_map/reduce-window
  19.8 6.2 %scatter_custom_fusion = s32[3072]{0:T(1024)S(1)} fusion(s32[1536]{0:T(1024)S(1)} %fusion.36, s32[1536]{0:T(1024)S(1)} %fusion.35, s32[]{:T(128)} %constant.19.clone.1), kind=kCustom, calls=%fused_computation.84 | custom fusion | bytes 12292 | tf_op jit(solution)/shard_map/scatter | solution.py:82
  26.7 7.3 %all-to-all-start = ((s32[32,1,96]{2,1,0:T(1,128)}), s32[32,1,96]{2,1,0:T(1,128)S(1)}, u32[]{:S(2)}, u32[]{:S(2)}) async-start(s32[32,1,96]{2,1,0:T(1,128)} %all_to_all.35), calls=%async_computation | async-start | bytes 32768 | tf_op jit(solution)/shard_map/all_to_all | solution.py:83
  34.1 1.8 copy.23
  35.9 5.7 %scatter_custom_fusion.1 = bf16[3072,128]{1,0:T(8,128)(2,1)} fusion(s32[1536]{0:T(1024)S(1)} %fusion.36, bf16[1536,128]{1,0:T(8,128)(2,1)} %param.9, bf16[]{:T(256)} %constant.24.clone.1), kind=kCustom, calls=%fused_computation.57 | custom fusion | bytes 786944 | tf_op jit(solution)/shard_map/scatter | solution.py:94
  41.6 3.9 %all-to-all-start.3 = ((bf16[2,192,256]{2,0,1:T(2,128)(2,1)}), bf16[2,192,256]{2,0,1:T(2,128)(2,1)S(1)}, u32[]{:S(2)}, u32[]{:S(2)}) async-start(bf16[2,192,256]{2,0,1:T(2,128)(2,1)} %copy.23), calls=%async_computation.3 | async-start | bytes 393216 | tf_op jit(solution)/shard_map/all_to_all | solution.py:121
  45.7 6.1 %all-to-all-done.3 = bf16[2,192,256]{2,0,1:T(2,128)(2,1)S(1)} async-done(((bf16[2,192,256]{2,0,1:T(2,128)(2,1)}), bf16[2,192,256]{2,0,1:T(2,128)(2,1)S(1)}, u32[]{:S(2)}, u32[]{:S(2)}) %all-to-all-start.3) | async-done | bytes 196640 | tf_op jit(solution)/shard_map/all_to_all | solution.py:121
  51.8 3.7 %all-to-all-start.1 = ((bf16[32,96,128]{2,1,0:T(8,128)(2,1)}), bf16[32,96,128]{2,1,0:T(8,128)(2,1)S(1)}, u32[]{:S(2)}, u32[]{:S(2)}) async-start(bf16[32,96,128]{2,1,0:T(8,128)(2,1)} %bitcast.4), calls=%async_computation.1 | async-start | bytes 1572864 | tf_op jit(solution)/shard_map/all_to_all | solution.py:96
  55.6 1.8 collective-permute-start.4
  57.4 2.1 collective-permute-start.5
  59.5 13.7 %collective-permute-done.4 = bf16[1,24,256]{2,1,0:T(8,128)(2,1)S(1)} collective-permute-done((bf16[1,24,256]{2,1,0:T(8,128)(2,1)S(1)}, bf16[1,24,256]{2,1,0:T(8,128)(2,1)S(1)}, u32[]{:S(2)}, u32[]{:S(2)}) %collective-permute-start.4) | collective-permute-done | bytes 12320 | tf_op jit(solution)/shard_map/ppermute | solution.py:17
  73.3 2.6 %collective-permute-start.7 = (bf16[18,1,256]{2,1,0:T(2,128)(2,1)S(1)}, bf16[18,1,256]{2,1,0:T(2,128)(2,1)S(1)}, u32[]{:S(2)}, u32[]{:S(2)}) collective-permute-start(bf16[18,1,256]{2,1,0:T(2,128)(2,1)S(1)} %get-tuple-element.29), channel_id=1, source_target_pairs={{1,0},{2,1},{3,2},{4,3},{5,4},{6,5},{7,6},{0,7},{9,8},{10,9},{11,1... | collective-permute-start | bytes 27656 | tf_op jit(solution)/shard_map/ppermute | solution.py:18
  77.9 11.1 %gather_fusion = bf16[3072,256]{1,0:T(8,128)(2,1)S(1)} fusion(bf16[385,256]{1,0:T(8,128)(2,1)S(1)} %concatenate.19, s32[3072]{0:T(1024)S(1)} %broadcast_clamp_fusion), kind=kCustom, calls=%fused_computation | custom fusion | bytes 3158016 | tf_op jit(solution)/shard_map/gather | solution.py:141
  89.0 2.3 fusion.45
  91.3 5.0 %convert_reduce_fusion = (f32[256]{0:T(256)S(1)}, bf16[3072,256]{1,0:T(8,128)(2,1)}, f32[3072,256]{1,0:T(8,128)S(1)}) fusion(f32[3072,256]{1,0:T(8,128)} %fusion.45, f32[256]{0:T(256)S(1)} %copy-done.4, bf16[3072,128]{1,0:T(8,128)(2,1)S(1)} %bitcast.78, bf16[128,256]{1,0:T(8,128)(2,1)S(1)} %copy-done.3), kind=kOutput, calls=%fused_computation.16 | convolution fusion | flops 219414272 | bytes 8718336 | tf_op jit(solution)/shard_map/dot_general | solution.py:24
  97.9 2.8 %fusion = f32[3072,256]{1,0:T(8,128)} fusion(bf16[256,256]{1,0:T(8,128)(2,1)S(1)} %copy-done, f32[3072,256]{1,0:T(8,128)S(1)} %get-tuple-element.41), kind=kOutput, calls=%fused_computation.8 | convolution fusion | flops 411303936 | bytes 6422528 | tf_op jit(solution)/shard_map/dot_general | solution.py:26
  100.7 19.6 %scatter_custom_fusion.2 = f32[385,256]{1,0:T(8,128)S(1)} fusion(s32[3072]{0:T(1024)S(1)} %reshape.214, f32[3072,256]{1,0:T(8,128)} %fusion, f32[]{:T(128)} %constant.18.clone.1), kind=kCustom, calls=%fused_computation.64 | custom fusion | flops 786432 | bytes 394752 | tf_op jit(solution)/shard_map/scatter-add | solution.py:105
  120.4 4.8 %collective-permute-start = (f32[1,24,256]{2,1,0:T(8,128)S(1)}, f32[1,24,256]{2,1,0:T(8,128)S(1)}, u32[]{:S(2)}, u32[]{:S(2)}) collective-permute-start(f32[1,24,256]{2,1,0:T(8,128)S(1)} %get-tuple-element.26), channel_id=1, source_target_pairs={{0,8},{8,16},{16,24},{24,0},{1,9},{9,17},{17,25},{25,1},{2,10},{10... | collective-permute-start | bytes 73736 | tf_op jit(solution)/shard_map/ppermute | solution.py:17
  125.2 3.9 %fusion.41 = f32[256,256]{1,0:T(8,128)} fusion(bf16[3072,256]{1,0:T(8,128)(2,1)S(1)} %gather_fusion, f32[3072,256]{1,0:T(8,128)} %copy-done.5), kind=kOutput, calls=%fused_computation.98 | convolution fusion | flops 409731072 | bytes 4980736 | tf_op jit(solution)/shard_map/dot_general | solution.py:32
  129.2 2.6 %collective-permute-start.3 = (f32[18,1,256]{2,1,0:T(1,128)S(1)}, f32[18,1,256]{2,1,0:T(1,128)S(1)}, u32[]{:S(2)}, u32[]{:S(2)}) collective-permute-start(f32[18,1,256]{2,1,0:T(1,128)S(1)} %get-tuple-element.25), channel_id=1, source_target_pairs={{1,0},{2,1},{3,2},{4,3},{5,4},{6,5},{7,6},{0,7},{9,8},{10,9},{11,1... | collective-permute-start | bytes 55304 | tf_op jit(solution)/shard_map/ppermute | solution.py:18
  134.7 3.9 %all-to-all-start.2 = ((bf16[16,24,256]{2,1,0:T(8,128)(2,1)}), bf16[16,24,256]{2,1,0:T(8,128)(2,1)S(1)}, u32[]{:S(2)}, u32[]{:S(2)}) async-start(bf16[16,24,256]{2,1,0:T(8,128)(2,1)} %add_convert_fusion), calls=%async_computation.2 | async-start | bytes 393216 | tf_op jit(solution)/shard_map/all_to_all | solution.py:117
  138.7 47.9 %all-reduce.8.cloned.1.call-done = (f32[128,256]{1,0:T(8,128)}, f32[256,256]{1,0:T(8,128)}) async-done(((f32[128,256]{1,0:T(8,128)}, f32[256,256]{1,0:T(8,128)}), (f32[128,256]{1,0:T(8,128)}, f32[256,256]{1,0:T(8,128)})) %all-reduce.8.cloned.1.call-update) | async-done | bytes 393232 | tf_op jit(solution)/shard_map/psum | solution.py:144
  186.7 22.4 %all-reduce.1 = (f32[256]{0:T(256)S(1)}, f32[9,256]{1,0:T(8,128)S(1)}) all-reduce(f32[256]{0:T(256)S(1)} %get-tuple-element.22, f32[9,256]{1,0:T(8,128)S(1)} %stack.2), channel_id=1, replica_groups=mesh['lat'=4,'lon'=8] {'lon'}, use_global_device_ids=true, to_apply=%region_9.10 | all-reduce | flops 2560 | bytes 20480 | tf_op jit(solution)/shard_map/psum | solution.py:144
  209.1 20.1 %all-reduce.3 = (f32[256]{0:T(256)}, f32[9,256]{1,0:T(8,128)}) all-reduce(f32[256]{0:T(256)S(1)} %get-tuple-element.14, f32[9,256]{1,0:T(8,128)S(1)} %get-tuple-element.15), channel_id=1, replica_groups=mesh['lat'=4,'lon'=8] {'lat'}, use_global_device_ids=true, to_apply=%region_10.11 | all-reduce | flops 2560 | bytes 20480 | tf_op jit(solution)/shard_map/psum | solution.py:143
  (72 shorter events, 14.5 us)
Async XLA Ops:
  7.2 81.8 %copy-start = (bf16[256,256]{1,0:T(8,128)(2,1)S(1)}, bf16[256,256]{1,0:T(8,128)(2,1)}, u32[]{:S(2)}) copy-start(bf16[256,256]{1,0:T(8,128)(2,1)} %param.15) | copy-start | bytes 393220
  7.2 38.4 %copy-start.2 = (f32[9,256]{1,0:T(8,128)S(1)}, f32[9,256]{1,0:T(8,128)}, u32[]{:S(2)}) copy-start(f32[9,256]{1,0:T(8,128)} %param.16) | copy-start | bytes 27652
  26.7 14.9 %all-to-all-start = ((s32[32,1,96]{2,1,0:T(1,128)}), s32[32,1,96]{2,1,0:T(1,128)S(1)}, u32[]{:S(2)}, u32[]{:S(2)}) async-start(s32[32,1,96]{2,1,0:T(1,128)} %all_to_all.35), calls=%async_computation | async-start | bytes 32768 | tf_op jit(solution)/shard_map/all_to_all | solution.py:83
  41.6 10.1 %all-to-all-start.3 = ((bf16[2,192,256]{2,0,1:T(2,128)(2,1)}), bf16[2,192,256]{2,0,1:T(2,128)(2,1)S(1)}, u32[]{:S(2)}, u32[]{:S(2)}) async-start(bf16[2,192,256]{2,0,1:T(2,128)(2,1)} %copy.23), calls=%async_computation.3 | async-start | bytes 393216 | tf_op jit(solution)/shard_map/all_to_all | solution.py:121
  51.8 39.5 %all-to-all-start.1 = ((bf16[32,96,128]{2,1,0:T(8,128)(2,1)}), bf16[32,96,128]{2,1,0:T(8,128)(2,1)S(1)}, u32[]{:S(2)}, u32[]{:S(2)}) async-start(bf16[32,96,128]{2,1,0:T(8,128)(2,1)} %bitcast.4), calls=%async_computation.1 | async-start | bytes 1572864 | tf_op jit(solution)/shard_map/all_to_all | solution.py:96
  55.5 131.1 %all-reduce.8.cloned.1.call-start = ((), (), s32[]{:S(2)}) async-start(), calls=%async_computation.4 | async-start | bytes 786432 | tf_op jit(solution)/shard_map/psum | solution.py:144
  55.6 17.6 %collective-permute-start.4 = (bf16[1,24,256]{2,1,0:T(8,128)(2,1)S(1)}, bf16[1,24,256]{2,1,0:T(8,128)(2,1)S(1)}, u32[]{:S(2)}, u32[]{:S(2)}) collective-permute-start(bf16[1,24,256]{2,1,0:T(8,128)(2,1)S(1)} %get-tuple-element.30), channel_id=1, source_target_pairs={{0,8},{8,16},{16,24},{24,0},{1,9},{9,17},{17,25},{25,1},{2,10},{10... | collective-permute-start | bytes 36872 | tf_op jit(solution)/shard_map/ppermute | solution.py:17
  57.4 15.8 %collective-permute-start.5 = (bf16[1,24,256]{2,1,0:T(8,128)(2,1)S(1)}, bf16[1,24,256]{2,1,0:T(8,128)(2,1)S(1)}, u32[]{:S(2)}, u32[]{:S(2)}) collective-permute-start(bf16[1,24,256]{2,1,0:T(8,128)(2,1)S(1)} %get-tuple-element.31), channel_id=1, source_target_pairs={{8,0},{16,8},{24,16},{0,24},{9,1},{17,9},{25,17},{1,25},{10,2},{18... | collective-permute-start | bytes 36872 | tf_op jit(solution)/shard_map/ppermute | solution.py:18
  73.3 4.1 %collective-permute-start.6 = (bf16[18,1,256]{2,1,0:T(2,128)(2,1)S(1)}, bf16[18,1,256]{2,1,0:T(2,128)(2,1)S(1)}, u32[]{:S(2)}, u32[]{:S(2)}) collective-permute-start(bf16[18,1,256]{2,1,0:T(2,128)(2,1)S(1)} %get-tuple-element.28), channel_id=1, source_target_pairs={{0,1},{1,2},{2,3},{3,4},{4,5},{5,6},{6,7},{7,0},{8,9},{9,10},{10,1... | collective-permute-start | bytes 27656 | tf_op jit(solution)/shard_map/ppermute | solution.py:17
  73.3 4.1 %collective-permute-start.7 = (bf16[18,1,256]{2,1,0:T(2,128)(2,1)S(1)}, bf16[18,1,256]{2,1,0:T(2,128)(2,1)S(1)}, u32[]{:S(2)}, u32[]{:S(2)}) collective-permute-start(bf16[18,1,256]{2,1,0:T(2,128)(2,1)S(1)} %get-tuple-element.29), channel_id=1, source_target_pairs={{1,0},{2,1},{3,2},{4,3},{5,4},{6,5},{7,6},{0,7},{9,8},{10,9},{11,1... | collective-permute-start | bytes 27656 | tf_op jit(solution)/shard_map/ppermute | solution.py:18
  89.0 2.3 copy-start.3
  89.0 2.3 copy-start.4
  96.2 1.7 copy-start.5
  120.4 8.7 %collective-permute-start = (f32[1,24,256]{2,1,0:T(8,128)S(1)}, f32[1,24,256]{2,1,0:T(8,128)S(1)}, u32[]{:S(2)}, u32[]{:S(2)}) collective-permute-start(f32[1,24,256]{2,1,0:T(8,128)S(1)} %get-tuple-element.26), channel_id=1, source_target_pairs={{0,8},{8,16},{16,24},{24,0},{1,9},{9,17},{17,25},{25,1},{2,10},{10... | collective-permute-start | bytes 73736 | tf_op jit(solution)/shard_map/ppermute | solution.py:17
  125.2 6.7 %copy-start.1 = (bf16[3072,256]{1,0:T(8,128)(2,1)S(1)}, bf16[3072,256]{1,0:T(8,128)(2,1)}, u32[]{:S(2)}) copy-start(bf16[3072,256]{1,0:T(8,128)(2,1)} %get-tuple-element.23) | copy-start | bytes 4718596
  125.2 3.9 %collective-permute-start.1 = (f32[1,24,256]{2,1,0:T(8,128)S(1)}, f32[1,24,256]{2,1,0:T(8,128)S(1)}, u32[]{:S(2)}, u32[]{:S(2)}) collective-permute-start(f32[1,24,256]{2,1,0:T(8,128)S(1)} %get-tuple-element.27), channel_id=1, source_target_pairs={{8,0},{16,8},{24,16},{0,24},{9,1},{17,9},{25,17},{1,25},{10,2},{18... | collective-permute-start | bytes 73736 | tf_op jit(solution)/shard_map/ppermute | solution.py:18
  129.1 4.1 %collective-permute-start.2 = (f32[18,1,256]{2,1,0:T(1,128)S(1)}, f32[18,1,256]{2,1,0:T(1,128)S(1)}, u32[]{:S(2)}, u32[]{:S(2)}) collective-permute-start(f32[18,1,256]{2,1,0:T(1,128)S(1)} %get-tuple-element.24), channel_id=1, source_target_pairs={{0,1},{1,2},{2,3},{3,4},{4,5},{5,6},{6,7},{7,0},{8,9},{9,10},{10,1... | collective-permute-start | bytes 55304 | tf_op jit(solution)/shard_map/ppermute | solution.py:17
  129.2 4.1 %collective-permute-start.3 = (f32[18,1,256]{2,1,0:T(1,128)S(1)}, f32[18,1,256]{2,1,0:T(1,128)S(1)}, u32[]{:S(2)}, u32[]{:S(2)}) collective-permute-start(f32[18,1,256]{2,1,0:T(1,128)S(1)} %get-tuple-element.25), channel_id=1, source_target_pairs={{1,0},{2,1},{3,2},{4,3},{5,4},{6,5},{7,6},{0,7},{9,8},{10,9},{11,1... | collective-permute-start | bytes 55304 | tf_op jit(solution)/shard_map/ppermute | solution.py:18
  134.7 94.5 %all-to-all-start.2 = ((bf16[16,24,256]{2,1,0:T(8,128)(2,1)}), bf16[16,24,256]{2,1,0:T(8,128)(2,1)S(1)}, u32[]{:S(2)}, u32[]{:S(2)}) async-start(bf16[16,24,256]{2,1,0:T(8,128)(2,1)} %add_convert_fusion), calls=%async_computation.2 | async-start | bytes 393216 | tf_op jit(solution)/shard_map/all_to_all | solution.py:117
  138.6 91.3 %all-reduce.10.cloned.1.call-start = ((), (), s32[]{:S(2)}) async-start(), calls=%async_computation.5 | async-start | bytes 786432 | tf_op jit(solution)/shard_map/psum | solution.py:143
Sparse Core Ops, SparseCore 0:
  133.1 53.5 all-reduce.7
  189.0 36.7 all-reduce.9
